TPU v7x, 512 devices: a whole 4x8x8 slice. The times are simulated.
512 devices in a mesh: tm: 2 (over y_lo), space: 64 (over y_hi, z, core), member: 4 (over x).
Axes of the slice: x: 4, y: 8 (y_hi: 4, y_lo: 2; y = y_hi * 2 + y_lo), z: 8, core: 2. Of those that a mesh axis runs over, the one named last changes fastest.
Arguments:
- obs_anom: bfloat16 [6, 2, 128, 256, 1024], P('tm', None, 'space', 'member'), may hold values from -0.59375 to 0.59375
- obs_prec: bfloat16 [6, 2, 128, 1024], P('tm', None, 'space'), may hold values from 0.29882812 to 3
- innov: bfloat16 [6, 2, 128, 1024], P('tm', None, 'space'), may hold values from -6 to 6
- obs_column: int32 [6, 2, 128, 1024], P('tm', None, 'space'), may hold values from 0 to 127
- cutoff: int32 [2, 128], replicated, may hold values from 1 to 2
- inv_root: float32 [2, 128, 256, 256], P('tm', 'space'), may hold values from -0.12 to 0.12
- state_anom: bfloat16 [2, 128, 256, 32, 128], P('tm', 'space', None, 'member'), may hold values from -6 to 6
- state_mean: float32 [2, 128, 32, 128], P('tm', 'space', 'member'), may hold values from -6 to 6
Outputs:
- analysis: bfloat16 [2, 128, 256, 32, 128], P('tm', 'space', None, 'member')
All inputs are finite; a program needn't handle non-finite values.
Results may differ from a plain program's by a relative error of at most 0.0062.
Values may be sent and summed in bfloat16 or wider, within the bound.
A program may use at most 64 MiB of HBM per device.

v0:
```python
import math

import jax
import jax.numpy as jnp
from jax import lax
from jax.sharding import PartitionSpec as P

K = 256
HALO = 2
NEWTON = 2


def cut_along(value, dim, count):
    before, after = (value.shape[:dim], value.shape[dim + 1 :])
    return jnp.moveaxis(value.reshape(*before, count, -1, *after), dim, 0)


def cut_rows(length, count):
    lap = length // count
    if lap >= 8:
        lap -= lap % 8
    return [lap * k for k in range(1, count)]


def in_order(tiles, dim):
    tiles = jnp.moveaxis(tiles, 0, dim)
    lengths = tiles.shape
    return tiles.reshape(*lengths[:dim], lengths[dim] * lengths[dim + 1], *lengths[dim + 2 :])


def cut_exchange(value, axis, pieces, split_dim, concat_dim):
    tiles = cut_along(value, split_dim, lax.axis_size(axis))
    split_at = max(range(1, max(2, tiles.ndim - 1)), key=lambda d: tiles.shape[d])
    done = []
    for share in jnp.split(tiles, cut_rows(tiles.shape[split_at], pieces), axis=split_at):
        if share.size:
            done.append(lax.all_to_all(share, axis, split_axis=0, concat_axis=0, tiled=True))
    return in_order(jnp.concatenate(done, axis=split_at), concat_dim)


def with_halo(value, sides, width):
    edges = {}
    for axis, dim in sides:
        count, length = (lax.axis_size(axis), value.shape[dim])
        up = [(i, (i + 1) % count) for i in range(count)]
        last = lax.slice_in_dim(value, length - width, length, axis=dim)
        initial = lax.slice_in_dim(value, 0, width, axis=dim)
        edges[dim] = (
            lax.ppermute(last, axis, up),
            lax.ppermute(initial, axis, [(b, a) for a, b in up]),
        )
    done = []
    for _, dim in sides:
        low, high = edges[dim]
        around = [(width, width) if d in done else (0, 0) for d in range(value.ndim)]
        value = jnp.concatenate([jnp.pad(low, around), value, jnp.pad(high, around)], axis=dim)
        done.append(dim)
    return value


def from_everyone(value, axis):
    copies = jnp.broadcast_to(value, (lax.axis_size(axis), *value.shape))
    return lax.all_to_all(copies, axis, split_axis=0, concat_axis=0, tiled=True)


def of_everyone(value, axis):
    everything = from_everyone(value, axis)
    return jnp.sum(everything, axis=0)


def packed_total(arrays, axis):
    flat, at, done = (jnp.concatenate([a.reshape(-1) for a in arrays]), 0, [])
    so_far = of_everyone(flat, axis)
    for a in arrays:
        done.append(so_far[at : at + a.size].reshape(a.shape))
        at += a.size
    return tuple(done)


def taper_weight(distance, reach_now, columns):
    scaled_reach = (reach_now + 0.5) * columns
    relative = distance / scaled_reach
    return jnp.square(jnp.maximum(1.0 - relative * relative, 0.0))


def tile_cutoffs(cutoff, first_tile, how_many):
    flattened = cutoff.reshape(-1)
    cycle_size = flattened.shape[0]
    wanted = (first_tile + jnp.arange(how_many, dtype=jnp.int32) + cycle_size) % cycle_size
    matches = wanted[:, None] == jnp.arange(cycle_size, dtype=jnp.int32)[None, :]
    return jnp.sum(jnp.where(matches, flattened[None, :], 0), axis=1).astype(jnp.float32)


def spread_sums(relaid, reaches, shifts, columns):
    members = relaid.shape[2] - 3
    tile_count = relaid.shape[1]
    window_len = shifts.shape[0]
    extended = tile_count + window_len - 1
    start_gram = jnp.zeros((extended, members, members), jnp.float32)
    start_proj = jnp.zeros((extended, members), jnp.float32)

    def add_tile(tile_index, carry):
        gram_sums, proj_sums = carry
        obs_slab = lax.dynamic_index_in_dim(relaid, tile_index, 1, keepdims=False)
        anomaly = obs_slab[:, :members]
        precision = obs_slab[:, members].astype(jnp.float32)
        innovation = obs_slab[:, members + 1].astype(jnp.float32)
        placing = obs_slab[:, members + 2].astype(jnp.float32)
        reach_now = lax.dynamic_slice_in_dim(reaches, tile_index, window_len, 0)
        distance = shifts[:, None, None] * columns + placing[None]
        coeffs = taper_weight(distance, reach_now[:, None, None], columns) * precision[None]
        scaled = (anomaly[None] * coeffs[:, :, None, :]).astype(jnp.bfloat16)
        weighted = (coeffs * innovation[None]).astype(jnp.bfloat16)
        gram_part = jnp.einsum("wsko,slo->wkl", scaled, anomaly, preferred_element_type=jnp.float32)
        proj_part = jnp.einsum("sko,wso->wk", anomaly, weighted, preferred_element_type=jnp.float32)
        gram_sums = lax.dynamic_update_slice_in_dim(
            gram_sums,
            lax.dynamic_slice_in_dim(gram_sums, tile_index, window_len, 0) + gram_part,
            tile_index,
            0,
        )
        proj_sums = lax.dynamic_update_slice_in_dim(
            proj_sums,
            lax.dynamic_slice_in_dim(proj_sums, tile_index, window_len, 0) + proj_part,
            tile_index,
            0,
        )
        return (gram_sums, proj_sums)

    return lax.fori_loop(0, tile_count, add_tile, (start_gram, start_proj))


def body(obs_anom, obs_prec, innov, obs_column, cutoff, inv_root, state_anom, state_mean):
    columns = state_anom.shape[-1]
    placing = (obs_column.astype(jnp.float32) + (0.5 - columns / 2)).astype(jnp.bfloat16)
    obs_info = jnp.stack([obs_prec, innov, placing], axis=3)
    quarter = obs_anom.shape[4] // lax.axis_size("member")
    own_part = lax.dynamic_slice_in_dim(obs_info, lax.axis_index("member") * quarter, quarter, 4)
    ensemble = cut_exchange(obs_anom, "member", 2, 4, 3)
    combined = jnp.concatenate([ensemble, own_part], axis=3)
    relaid = lax.all_to_all(combined, "tm", split_axis=1, concat_axis=0, tiled=True)[:, 0]
    tile_count = relaid.shape[1]
    first_tile = (
        lax.axis_index("tm") * lax.axis_size("space") + lax.axis_index("space")
    ) * tile_count
    window_len = 2 * HALO + 1
    reaches = tile_cutoffs(cutoff, first_tile - HALO, tile_count + 2 * HALO)
    shifts = (HALO - jnp.arange(window_len, dtype=jnp.int32)).astype(jnp.float32)
    ext_gram, ext_proj = spread_sums(relaid, reaches, shifts, columns)
    stacked = jnp.concatenate([ext_gram, ext_proj[:, None, :]], axis=1)
    outgoing = jnp.concatenate([stacked[:HALO], stacked[tile_count + HALO :]], axis=0)
    arrived = with_halo(outgoing.astype(jnp.bfloat16), ((("tm", "space"), 0),), HALO).astype(
        outgoing.dtype
    )
    owned = stacked[HALO : HALO + tile_count]
    owned = owned.at[:HALO].add(arrived[:HALO])
    owned = owned.at[tile_count - HALO :].add(arrived[3 * HALO :])
    gram_sums = owned[:, :K]
    proj_sums = owned[:, K]
    gram_sums, proj_sums = packed_total((gram_sums, proj_sums), "member")
    highest = lax.Precision.HIGHEST
    identity = jnp.eye(K, dtype=jnp.float32)
    system = (K - 1.0) * identity + gram_sums
    inv_sqrt = inv_root[0]
    for newton_step in range(NEWTON):
        square = jnp.einsum("tij,tjk->tik", inv_sqrt, inv_sqrt, precision=highest)
        applied = jnp.einsum("tij,tjk->tik", system, square, precision=highest)
        inv_sqrt = 1.5 * inv_sqrt - 0.5 * jnp.einsum(
            "tij,tjk->tik", inv_sqrt, applied, precision=highest
        )
    inner_prod = jnp.einsum("tij,tj->ti", inv_sqrt, proj_sums, precision=highest)
    mean_weight = jnp.einsum("tij,tj->ti", inv_sqrt, inner_prod, precision=highest)
    weights = (mean_weight[:, :, None] + math.sqrt(K - 1) * inv_sqrt).astype(jnp.bfloat16)
    anomalies = state_anom[0].reshape(tile_count, K, -1)
    mean_rows = state_mean[0].reshape(tile_count, 1, -1)
    result = (
        jnp.einsum("tij,tiq->tjq", weights, anomalies, preferred_element_type=jnp.float32)
        + mean_rows
    )
    return result.astype(jnp.bfloat16).reshape(state_anom.shape)


def solution(mesh):
    in_specs = (
        P("tm", None, "space", "member", None),
        P("tm", None, "space", None),
        P("tm", None, "space", None),
        P("tm", None, "space", None),
        P(),
        P("tm", "space", None, None),
        P("tm", "space", None, "member", None),
        P("tm", "space", "member", None),
    )
    out_specs = P("tm", "space", None, "member", None)
    return jax.shard_map(body, mesh=mesh, in_specs=in_specs, out_specs=out_specs, check_vma=False)
```

profile of v0, /device:TPU:32, one launch (start us, length us, event | category | flops | bytes accessed | tf_op | source)
XLA Modules:
  0.0 127.6 jit_solution(7590657255504218693)
XLA Ops:
  0.0 2.9 %reshape.165 = bf16[3,2,2,64,4,256]{5,4,3,2,1,0:T(4,128)(2,1)S(1)} reshape(bf16[3,2,2,64,1024]{4,3,2,1,0:T(8,128)(2,1)} %param.18) | data formatting | bytes 3145728 | tf_op jit(solution)/shard_map/reshape | solution.py:15
  4.5 4.3 %all-to-all-start = ((bf16[4,3,2,2,32,256]{5,4,3,2,1,0:T(8,128)(2,1)}), bf16[4,3,2,2,32,256]{5,4,3,2,1,0:T(8,128)(2,1)S(1)}, u32[]{:S(2)}, u32[]{:S(2)}) async-start(bf16[4,3,2,2,32,256]{5,4,3,2,1,0:T(8,128)(2,1)} %copy.91), calls=%async_computation | async-start | bytes 1572864 | tf_op jit(solution)/shard_map/all_to_all | solution.py:37
  9.8 11.3 %all-to-all-done = bf16[4,3,2,2,32,256]{5,4,3,2,1,0:T(8,128)(2,1)S(1)} async-done(((bf16[4,3,2,2,32,256]{5,4,3,2,1,0:T(8,128)(2,1)}), bf16[4,3,2,2,32,256]{5,4,3,2,1,0:T(8,128)(2,1)S(1)}, u32[]{:S(2)}, u32[]{:S(2)}) %all-to-all-start) | async-done | bytes 786464 | tf_op jit(solution)/shard_map/all_to_all | solution.py:37
  21.1 3.5 %all-to-all-start.1 = ((bf16[4,3,2,2,32,256]{5,4,3,2,1,0:T(8,128)(2,1)}), bf16[4,3,2,2,32,256]{5,4,3,2,1,0:T(8,128)(2,1)S(1)}, u32[]{:S(2)}, u32[]{:S(2)}) async-start(bf16[4,3,2,2,32,256]{5,4,3,2,1,0:T(8,128)(2,1)} %copy.92), calls=%async_computation.1 | async-start | bytes 1572864 | tf_op jit(solution)/shard_map/all_to_all | solution.py:37
  24.9 11.1 %all-to-all-done.1 = bf16[4,3,2,2,32,256]{5,4,3,2,1,0:T(8,128)(2,1)S(1)} async-done(((bf16[4,3,2,2,32,256]{5,4,3,2,1,0:T(8,128)(2,1)}), bf16[4,3,2,2,32,256]{5,4,3,2,1,0:T(8,128)(2,1)S(1)}, u32[]{:S(2)}, u32[]{:S(2)}) %all-to-all-start.1) | async-done | bytes 786464 | tf_op jit(solution)/shard_map/all_to_all | solution.py:37
  36.4 2.4 %copy.98 = bf16[3,2,2,259,256]{4,2,3,0,1:T(2,128)(2,1)} copy(bf16[3,2,2,259,256]{4,3,2,1,0:T(8,128)(2,1)S(1)} %pad_maximum_fusion) | data formatting | bytes 3182592 | tf_op jit(solution)/shard_map/concatenate | solution.py:140
  38.8 3.8 %all-to-all-start.2 = ((bf16[3,2,2,259,256]{4,2,3,0,1:T(2,128)(2,1)}), bf16[3,2,2,259,256]{4,2,3,0,1:T(2,128)(2,1)S(1)}, u32[]{:S(2)}, u32[]{:S(2)}) async-start(bf16[3,2,2,259,256]{4,2,3,0,1:T(2,128)(2,1)} %copy.98), calls=%async_computation.2 | async-start | bytes 3182592 | tf_op jit(solution)/shard_map/all_to_all | solution.py:141
  42.8 17.2 %all-to-all-done.2 = bf16[3,2,2,259,256]{4,2,3,0,1:T(2,128)(2,1)S(1)} async-done(((bf16[3,2,2,259,256]{4,2,3,0,1:T(2,128)(2,1)}), bf16[3,2,2,259,256]{4,2,3,0,1:T(2,128)(2,1)S(1)}, u32[]{:S(2)}, u32[]{:S(2)}) %all-to-all-start.2) | async-done | bytes 1591328 | tf_op jit(solution)/shard_map/all_to_all | solution.py:141
  60.0 1.2 copy-done
  61.1 1.6 %copy.99 = bf16[6,2,259,256]{3,2,0,1:T(8,128)(2,1)S(1)} copy(bf16[6,2,259,256]{3,1,2,0:T(2,128)(2,1)} %bitcast.100) | data formatting | bytes 3182592
  62.9 4.5 %while.20 = (s32[]{:T(128)}, f32[6,256,256]{2,1,0:T(8,128)S(1)}, f32[6,256]{1,0:T(8,128)S(1)}, bf16[6,2,259,256]{3,2,0,1:T(8,128)(2,1)S(1)}, f32[6]{0:T(128)S(1)}, /*index=5*/s32[]{:T(128)}, s32[]{:T(128)}) while((s32[]{:T(128)}, f32[6,256,256]{2,1,0:T(8,128)S(1)}, f32[6,256]{1,0:T(8,128)S(1)}, ...), condition=%wide.region_2.3_spmd.clone, body=%wide.region_1.2_spmd.clone.sunk | while | flops 1015346944 | bytes 9977029 | solution.py:130
  63.4 1.3 %fusion.59 = f32[6,256,256]{2,1,0:T(8,128)S(1)} fusion(f32[6,256,256]{2,1,0:T(8,128)S(1)} %get-tuple-element.268, s32[]{:T(128)} %get-tuple-element.267, f32[5,6,256]{2,1,0:T(8,128)S(1)} %copy.157, f32[6,256,256]{2,1,0:T(8,128)S(1)} %slice_convert_fusion.7, bf16[6,259,256]{2,1,0:T(8,128)(2,1)S(1)} %dynamic-slice_bitcast_fusion.2), kind=kOutput, calls=%fused_computation.7.clone.1 | convolution fusion | flops 1010892800 | bytes 5021700 | tf_op jit(solution)/shard_map/while/body/eval_jaxpr/wsko,slo->wkl/dot_general | solution.py:114
  65.6 1.3 %fusion.59 = f32[6,256,256]{2,1,0:T(8,128)S(1)} fusion(f32[6,256,256]{2,1,0:T(8,128)S(1)} %get-tuple-element.268, s32[]{:T(128)} %get-tuple-element.267, f32[5,6,256]{2,1,0:T(8,128)S(1)} %copy.157, f32[6,256,256]{2,1,0:T(8,128)S(1)} %slice_convert_fusion.7, bf16[6,259,256]{2,1,0:T(8,128)(2,1)S(1)} %dynamic-slice_bitcast_fusion.2), kind=kOutput, calls=%fused_computation.7.clone.1 | convolution fusion | flops 1010892800 | bytes 5021700 | tf_op jit(solution)/shard_map/while/body/eval_jaxpr/wsko,slo->wkl/dot_general | solution.py:114
  67.7 1.9 %collective-permute-start = (bf16[2,257,256]{2,1,0:T(8,128)(2,1)S(1)}, bf16[2,257,256]{2,1,0:T(8,128)(2,1)S(1)}, u32[]{:S(2)}, u32[]{:S(2)}) collective-permute-start(bf16[2,257,256]{2,1,0:T(8,128)(2,1)S(1)} %get-tuple-element.213), channel_id=1, source_target_pairs={{0,4},{4,8},{8,12},{12,16},{16,20},{20,24},{24,28},{28,32},{32,36}... | collective-permute-start | bytes 789512 | tf_op jit(solution)/shard_map/ppermute | solution.py:49
  69.7 7.9 %collective-permute-start.1 = (bf16[2,257,256]{2,1,0:T(8,128)(2,1)S(1)}, bf16[2,257,256]{2,1,0:T(8,128)(2,1)S(1)}, u32[]{:S(2)}, u32[]{:S(2)}) collective-permute-start(bf16[2,257,256]{2,1,0:T(8,128)(2,1)S(1)} %get-tuple-element.214), channel_id=1, source_target_pairs={{4,0},{8,4},{12,8},{16,12},{20,16},{24,20},{28,24},{32,28},{36,32}... | collective-permute-start | bytes 789512 | tf_op jit(solution)/shard_map/ppermute | solution.py:50
  77.5 4.2 %collective-permute-done = bf16[2,257,256]{2,1,0:T(8,128)(2,1)S(1)} collective-permute-done((bf16[2,257,256]{2,1,0:T(8,128)(2,1)S(1)}, bf16[2,257,256]{2,1,0:T(8,128)(2,1)S(1)}, u32[]{:S(2)}, u32[]{:S(2)}) %collective-permute-start) | collective-permute-done | bytes 263200 | tf_op jit(solution)/shard_map/ppermute | solution.py:49
  81.7 2.4 %collective-permute-done.1 = bf16[2,257,256]{2,1,0:T(8,128)(2,1)S(1)} collective-permute-done((bf16[2,257,256]{2,1,0:T(8,128)(2,1)S(1)}, bf16[2,257,256]{2,1,0:T(8,128)(2,1)S(1)}, u32[]{:S(2)}, u32[]{:S(2)}) %collective-permute-start.1) | collective-permute-done | bytes 263200 | tf_op jit(solution)/shard_map/ppermute | solution.py:50
  84.6 3.5 %broadcast_in_dim.57 = f32[4,1,131584]{2,1,0:T(1,128)} broadcast(f32[131584]{0:T(1024)S(1)} %pad_maximum_fusion.2), dimensions={2} | broadcast | bytes 2631680 | tf_op jit(solution)/shard_map/broadcast_in_dim | solution.py:62
  88.1 3.9 %all-to-all-start.3 = ((f32[4,1,131584]{2,1,0:T(1,128)}), f32[4,1,131584]{2,1,0:T(1,128)S(1)}, u32[]{:S(2)}, u32[]{:S(2)}) async-start(f32[4,1,131584]{2,1,0:T(1,128)} %broadcast_in_dim.57), calls=%async_computation.3 | async-start | bytes 4210688 | tf_op jit(solution)/shard_map/all_to_all | solution.py:63
  93.0 2.3 %reshape_squeeze.8 = bf16[2,256,1024]{2,1,0:T(8,128)(2,1)} reshape(bf16[1,2,256,8,128]{4,3,2,1,0:T(8,128)(2,1)} %param.24) | data formatting | bytes 2097152 | tf_op jit(solution)/shard_map/reshape;squeeze | solution.py:174
  95.4 1.5 %fusion.19 = f32[2,256,256]{2,1,0:T(8,128)} fusion(f32[1,2,256,256]{3,2,1,0:T(8,128)S(1)} %copy-done.1), kind=kOutput, calls=%fused_computation.39 | convolution fusion | flops 402653184 | bytes 1048576 | tf_op jit(solution)/shard_map/tij,tjk->tik/dot_general | solution.py:166
  96.8 17.9 %all-to-all-done.3 = f32[4,1,131584]{2,1,0:T(1,128)S(1)} async-done(((f32[4,1,131584]{2,1,0:T(1,128)}), f32[4,1,131584]{2,1,0:T(1,128)S(1)}, u32[]{:S(2)}, u32[]{:S(2)}) %all-to-all-start.3) | async-done | bytes 2105376 | tf_op jit(solution)/shard_map/all_to_all | solution.py:63
  114.7 4.4 %reduce_sum.19 = f32[131584]{0:T(1024)S(1)} reduce(f32[4,1,131584]{2,1,0:T(1,128)S(1)} %all-to-all-done.3, f32[]{:T(128)} %constant.160.clone.1), dimensions={0,1}, to_apply=%region_3.4 | reduce | flops 394752 | bytes 2631684 | tf_op jit(solution)/shard_map/reduce_sum | solution.py:68
  126.3 1.2 copy.139
  (84 shorter events, 14.1 us)
Async XLA Ops:
  4.5 16.6 %all-to-all-start = ((bf16[4,3,2,2,32,256]{5,4,3,2,1,0:T(8,128)(2,1)}), bf16[4,3,2,2,32,256]{5,4,3,2,1,0:T(8,128)(2,1)S(1)}, u32[]{:S(2)}, u32[]{:S(2)}) async-start(bf16[4,3,2,2,32,256]{5,4,3,2,1,0:T(8,128)(2,1)} %copy.91), calls=%async_computation | async-start | bytes 1572864 | tf_op jit(solution)/shard_map/all_to_all | solution.py:37
  8.8 15.8 %copy-start.6 = (s32[3,2,2,1024]{3,2,1,0:T(2,128)S(1)}, s32[3,2,2,1024]{3,2,1,0:T(2,128)}, u32[]{:S(2)}) copy-start(s32[3,2,2,1024]{3,2,1,0:T(2,128)} %param.21) | copy-start | bytes 147460
  8.8 15.9 %copy-start.7 = (bf16[3,2,2,1024]{3,2,1,0:T(2,128)(2,1)S(1)}, bf16[3,2,2,1024]{3,2,1,0:T(2,128)(2,1)}, u32[]{:S(2)}) copy-start(bf16[3,2,2,1024]{3,2,1,0:T(2,128)(2,1)} %param.19) | copy-start | bytes 73732
  8.8 15.9 %copy-start.8 = (bf16[3,2,2,1024]{3,2,1,0:T(2,128)(2,1)S(1)}, bf16[3,2,2,1024]{3,2,1,0:T(2,128)(2,1)}, u32[]{:S(2)}) copy-start(bf16[3,2,2,1024]{3,2,1,0:T(2,128)(2,1)} %param.20) | copy-start | bytes 73732
  21.1 14.9 %all-to-all-start.1 = ((bf16[4,3,2,2,32,256]{5,4,3,2,1,0:T(8,128)(2,1)}), bf16[4,3,2,2,32,256]{5,4,3,2,1,0:T(8,128)(2,1)S(1)}, u32[]{:S(2)}, u32[]{:S(2)}) async-start(bf16[4,3,2,2,32,256]{5,4,3,2,1,0:T(8,128)(2,1)} %copy.92), calls=%async_computation.1 | async-start | bytes 1572864 | tf_op jit(solution)/shard_map/all_to_all | solution.py:37
  38.8 3.8 %copy-start.10 = (s32[2,128]{1,0:T(2,128)S(1)}, s32[2,128]{1,0:T(2,128)}, u32[]{:S(2)}) copy-start(s32[2,128]{1,0:T(2,128)} %param.22) | copy-start | bytes 3076
  38.8 21.2 %all-to-all-start.2 = ((bf16[3,2,2,259,256]{4,2,3,0,1:T(2,128)(2,1)}), bf16[3,2,2,259,256]{4,2,3,0,1:T(2,128)(2,1)S(1)}, u32[]{:S(2)}, u32[]{:S(2)}) async-start(bf16[3,2,2,259,256]{4,2,3,0,1:T(2,128)(2,1)} %copy.98), calls=%async_computation.2 | async-start | bytes 3182592 | tf_op jit(solution)/shard_map/all_to_all | solution.py:141
  60.0 1.2 copy-start
  67.7 14.0 %collective-permute-start = (bf16[2,257,256]{2,1,0:T(8,128)(2,1)S(1)}, bf16[2,257,256]{2,1,0:T(8,128)(2,1)S(1)}, u32[]{:S(2)}, u32[]{:S(2)}) collective-permute-start(bf16[2,257,256]{2,1,0:T(8,128)(2,1)S(1)} %get-tuple-element.213), channel_id=1, source_target_pairs={{0,4},{4,8},{8,12},{12,16},{16,20},{20,24},{24,28},{28,32},{32,36}... | collective-permute-start | bytes 789512 | tf_op jit(solution)/shard_map/ppermute | solution.py:49
  69.7 14.4 %collective-permute-start.1 = (bf16[2,257,256]{2,1,0:T(8,128)(2,1)S(1)}, bf16[2,257,256]{2,1,0:T(8,128)(2,1)S(1)}, u32[]{:S(2)}, u32[]{:S(2)}) collective-permute-start(bf16[2,257,256]{2,1,0:T(8,128)(2,1)S(1)} %get-tuple-element.214), channel_id=1, source_target_pairs={{4,0},{8,4},{12,8},{16,12},{20,16},{24,20},{28,24},{32,28},{36,32}... | collective-permute-start | bytes 789512 | tf_op jit(solution)/shard_map/ppermute | solution.py:50
  88.1 3.9 %copy-start.1 = (f32[1,2,256,256]{3,2,1,0:T(8,128)S(1)}, f32[1,2,256,256]{3,2,1,0:T(8,128)}, u32[]{:S(2)}) copy-start(f32[1,2,256,256]{3,2,1,0:T(8,128)} %param.23) | copy-start | bytes 1572868
  88.1 26.7 %all-to-all-start.3 = ((f32[4,1,131584]{2,1,0:T(1,128)}), f32[4,1,131584]{2,1,0:T(1,128)S(1)}, u32[]{:S(2)}, u32[]{:S(2)}) async-start(f32[4,1,131584]{2,1,0:T(1,128)} %broadcast_in_dim.57), calls=%async_computation.3 | async-start | bytes 4210688 | tf_op jit(solution)/shard_map/all_to_all | solution.py:63
  92.0 3.3 %copy-start.9 = (f32[1,2,8,128]{3,2,1,0:T(8,128)S(1)}, f32[1,2,8,128]{3,2,1,0:T(8,128)}, u32[]{:S(2)}) copy-start(f32[1,2,8,128]{3,2,1,0:T(8,128)} %param.25) | copy-start | bytes 24580
  119.2 2.3 %copy-start.3 = (f32[131584]{0:T(1024)}, f32[131584]{0:T(1024)S(1)}, u32[]{:S(2)}) copy-start(f32[131584]{0:T(1024)S(1)} %reduce_sum.19) | copy-start | bytes 1579012
  119.2 1.2 copy-start.4
  119.2 2.3 %copy-start.5 = (f32[1,2,256,256]{2,3,1,0:T(8,128)S(1)}, f32[1,2,256,256]{2,3,1,0:T(8,128)}, u32[]{:S(2)}) copy-start(f32[1,2,256,256]{2,3,1,0:T(8,128)} %copy.90) | copy-start | bytes 1572868
  123.3 1.8 %slice-start = ((f32[131584]{0:T(1024)}), f32[512]{0:T(512)S(1)}, s32[]{:S(2)}) async-start(f32[131584]{0:T(1024)} %copy-done.3), calls=%async_computation.4 | async-start | bytes 4096 | tf_op jit(solution)/shard_map/slice | solution.py:75
  124.0 1.9 %copy-start.2 = (bf16[2,256,1024]{2,1,0:T(8,128)(2,1)S(1)}, bf16[2,256,1024]{2,1,0:T(8,128)(2,1)}, u32[]{:S(2)}) copy-start(bf16[2,256,1024]{2,1,0:T(8,128)(2,1)} %reshape_squeeze.8) | copy-start | bytes 3145732
where the time goes:
time: 128 us
  waiting for transfers between devices  64 us (50%)
  starting transfers between devices  25.3 us (20%)
  local copies, waits for them, and re-layouts  21.2 us (17%)
  matrix products  10.6 us (8%)
  other arithmetic  5.88 us (5%)
    all_to_all x2, waiting for transfers between devices, cut_exchange(): lax.all_to_all(share, axis, split_axis=0, concat_axis=0, tiled=True)  22.3 us
    all_to_all x1, waiting for transfers between devices, from_everyone(): return lax.all_to_all(copies, axis, split_axis=0, concat_axis=0, tiled=True)  17.9 us
    all_to_all x1, waiting for transfers between devices, body(): lax.all_to_all(combined, 'tm', split_axis=1, concat_axis=0, tiled=True)  17.2 us
    ppermute x1, starting transfers between devices, with_halo(): lax.ppermute(initial, axis, [(b, a) for a, b in up])  7.86 us
    all_to_all x2, starting transfers between devices, cut_exchange(): lax.all_to_all(share, axis, split_axis=0, concat_axis=0, tiled=True)  7.79 us
    unnamed x28, local copies, waits for them, and re-layouts  6.51 us
    reduce_sum x1, other arithmetic, of_everyone(): return jnp.sum(everything, axis=0)  4.4 us
    ppermute x1, waiting for transfers between devices, with_halo(): lax.ppermute(last, axis, up)  4.16 us
  transfers between devices with their start and end apart: 6, of which 6 were waited for; matrix products, arithmetic and copies ran while one was open for 5% of the time, Pallas kernels for 0%

commit v1 on v0

v1 whole, which is shorter than its diff:
```python
import functools
import math

import jax
import jax.numpy as jnp
from jax import lax
from jax.experimental import pallas as pl
from jax.experimental.pallas import tpu as pltpu
from jax.sharding import PartitionSpec as P

MESH = pl.DeviceIdType.MESH
K = 256
POINTS = 128
NEWTON = 2
CHUNKS = 6
WIDTH = 512
WIN = 5
NEAR = 192
LATE = WIN * 64 + 16
F32 = jnp.float32
BF16 = jnp.bfloat16


def nt_dot(a, b):
    return lax.dot_general(a, b, (((1,), (1,)), ((), ())), preferred_element_type=F32)


def split(a):
    hi = a.astype(BF16)
    return hi, (a - hi.astype(F32)).astype(BF16)


def mm(a, b):
    return jnp.dot(a, b, preferred_element_type=F32)


def mm3(a, b):
    (ah, al), (bh, bl) = a, b
    return mm(ah, bh) + (mm(ah, bl) + mm(al, bh))


def gather_kernel(
    obs_ref, prec_ref, innov_ref, col_ref, cut_hbm, state_ref, root_hbm,
    gram_out, proj_out, flat_out, square_out,
    data, prec_v, innov_v, col_v, cut_ref, coef, wgt, lhs_e, lhs_f, acc_e, acc_f,
    send_e, got_e, send_f, got_f, send_p, got_p, all_e, all_f, all_p, strip, state_v, root_v, tmp,
    info_sem, state_sem, info_send, info_recv, a2a_send, a2a_recv,
    e_send, e_recv, f_send, f_recv, p_send, p_recv, eb_send, eb_recv, fb_send, fb_recv, pb_send, pb_recv,
):
    tm = lax.axis_index("tm")
    s = lax.axis_index("space")
    x = lax.axis_index("member")
    ns = 64
    i = lax.rem(x, 2)
    half = x // 2
    pair = tm * ns + s
    other = 1 - tm

    def pair_at(p):
        q = lax.rem(p + 2 * ns, 2 * ns)
        return {"tm": q // ns, "space": lax.rem(q, ns)}

    lower, upper = pair_at(pair - 1), pair_at(pair + 1)

    def peer(h, k):
        return {"tm": lax.rem(tm + h, 2), "member": lax.rem(x + k, 4)}

    place = {1: 0, 0: 1, 3: 2, 2: 3}

    own = [
        pltpu.make_async_copy(
            obs_ref.at[c, tm, i, :, pl.ds(pl.multiple_of(half * WIDTH, WIDTH), WIDTH)],
            data.at[c, 64:128, :],
            a2a_recv.at[0, 0, c],
        )
        for c in range(3)
    ]
    for cp in own:
        cp.start()
    infos = [(prec_ref, prec_v), (innov_ref, innov_v), (col_ref, col_v)]
    local = [pltpu.make_async_copy(a.at[:, tm], b.at[0], info_sem.at[n]) for n, (a, b) in enumerate(infos)]
    for cp in local:
        cp.start()
    cut_cp = pltpu.make_async_copy(cut_hbm, cut_ref, info_sem.at[3])
    cut_cp.start()
    state_cp = pltpu.make_async_copy(state_ref.at[0], state_v, state_sem)
    state_cp.start()
    root_cp = pltpu.make_async_copy(root_hbm.at[0], root_v, info_sem.at[4])
    root_cp.start()

    barrier = pltpu.get_barrier_semaphore()
    for h in range(2):
        for k in range(4):
            if h or k:
                pl.semaphore_signal(barrier, inc=1, device_id=peer(h, k), device_id_type=MESH)
    pl.semaphore_signal(barrier, inc=1, device_id=lower, device_id_type=MESH)
    pl.semaphore_signal(barrier, inc=1, device_id=upper, device_id_type=MESH)
    pl.semaphore_wait(barrier, 9)

    def remote(src, dst, send, recv, dev):
        return pltpu.make_async_remote_copy(
            src_ref=src, dst_ref=dst, send_sem=send, recv_sem=recv, device_id=dev, device_id_type=MESH
        )

    def await_into(dst, recv):
        remote(dst, dst, info_send.at[0], recv, lower).wait_recv()

    info_cps = [
        remote(a.at[:, other], b.at[1], info_send.at[n], info_recv.at[n], {"tm": other})
        for n, (a, b) in enumerate(infos)
    ]
    for cp in info_cps:
        cp.start()

    def a2a(h, k, c):
        xp = lax.rem(x + k, 4)
        return remote(
            obs_ref.at[
                c, lax.rem(tm + h, 2), lax.rem(xp, 2), :, pl.ds(pl.multiple_of((xp // 2) * WIDTH, WIDTH), WIDTH)
            ],
            data.at[3 * h + c, pl.ds(place[k] * 64, 64), :],
            a2a_send.at[h, k, c],
            a2a_recv.at[h, k, c],
            peer(h, k),
        )

    order = [(h, k, c) for c in range(3) for h, k in ((0, 1), (0, 3), (1, 0), (1, 1), (1, 3))]
    order += [(h, 2, c) for c in range(3) for h in range(2)]
    for args in order:
        a2a(*args).start()

    z6 = jnp.where(i == 0, 5, 0)
    send_e[z6] = jnp.zeros((NEAR, 128), BF16)
    send_f[z6] = jnp.zeros((64, 256), BF16)
    send_p[z6] = jnp.zeros((1, 256), F32)

    state_cp.wait()
    for t in range(2):

        def relay(n, carry, t=t):
            block = state_v[t, pl.ds(pl.multiple_of(n * 16, 16), 16)].astype(F32)
            tmp[...] = block.reshape(128, 128)
            for level in range(8):
                flat_out[t, pl.ds(pl.multiple_of(n * 16, 16), 16), level * 128 : (level + 1) * 128] = tmp[
                    pl.ds(level, 16, stride=8), :
                ].astype(BF16)
            return carry

        lax.fori_loop(0, 16, relay, 0)

    for cp in local + [cut_cp]:
        cp.wait()
    for n, (a, b) in enumerate(infos):
        await_into(b.at[1], info_recv.at[n])
    lanes = pl.ds(pl.multiple_of(half * WIDTH, WIDTH), WIDTH)
    for c in range(CHUNKS):

        def row(ref):
            both = ref[c // 3, c % 3, :, lanes].astype(F32)
            return jnp.where(i == 0, both[0:1], both[1:2])

        prec, innov, col = row(prec_v), row(innov_v), row(col_v)
        rows, wrows = [], []
        for w in range(WIN):
            target = lax.rem(2 * pair + i + w - 2 + 4 * ns, 4 * ns)
            reach = (cut_ref[target // (2 * ns), lax.rem(target, 2 * ns)].astype(F32) + 0.5) * POINTS
            relative = (col + ((2 - w) * POINTS + 0.5 - POINTS / 2)) / reach
            taper = jnp.maximum(1.0 - relative * relative, 0.0)
            cf = taper * taper * prec
            rows.append(cf)
            wrows.append(cf * innov)
        zero = jnp.zeros((1, WIDTH), F32)
        coef[c] = jnp.concatenate(rows + [zero] * 3, axis=0)
        wgt[c] = jnp.concatenate(wrows + [zero] * 11, axis=0).astype(BF16)

    root_cp.wait()
    for t in range(2):
        part = split(root_v[t])
        square_out[t] = mm3(part, part)

    acc_e[...] = jnp.zeros_like(acc_e)
    acc_f[...] = jnp.zeros_like(acc_f)

    def near(c, carry):
        h, sl = c // 3, lax.rem(c, 3)
        for k in (0, 1, 3):
            await_into(data.at[c, place[k] * 64 : place[k] * 64 + 64, :], a2a_recv.at[h, k, sl])
        for rb in range(6):
            rows = data[c, rb * 32 : (rb + 1) * 32, :].astype(F32)
            for w in range(WIN):
                lhs_e[w * NEAR + rb * 32 : w * NEAR + (rb + 1) * 32, :] = (rows * coef[c, w : w + 1, :]).astype(BF16)
        acc_e[:, 0:NEAR] += nt_dot(lhs_e[...], data[c, 0:NEAR, :])
        return carry

    lax.fori_loop(0, CHUNKS, near, 0)
    left = lax.broadcasted_iota(jnp.int32, (64, 128), 1) < 64
    for w in range(WIN):
        w6, b = i + w, w * NEAR
        send_e[w6, 0:64, :] = jnp.where(left, acc_e[b : b + 64, 0:128], acc_e[b + 64 : b + 128, 0:128]).astype(BF16)
        send_e[w6, 64:128, :] = jnp.where(
            left, acc_e[b + 64 : b + 128, 0:128], pltpu.roll(acc_e[b + 128 : b + 192, 128:256], 64, 1)
        ).astype(BF16)
        send_e[w6, 128:192, :] = acc_e[b + 128 : b + 192, 0:128].astype(BF16)

    e_cps = [
        remote(send_e.at[0:2], got_e.at[0], e_send.at[0], e_recv.at[0], lower),
        remote(send_e.at[4:6], got_e.at[1], e_send.at[1], e_recv.at[1], upper),
    ]
    for cp in e_cps:
        cp.start()
    def late(c, carry):
        h, sl = c // 3, lax.rem(c, 3)
        await_into(data.at[c, 192:256, :], a2a_recv.at[h, 2, sl])
        for rb in range(2):
            rows = data[c, NEAR + rb * 32 : NEAR + (rb + 1) * 32, :].astype(F32)
            for w in range(WIN):
                lhs_f[w * 64 + rb * 32 : w * 64 + (rb + 1) * 32, :] = (rows * coef[c, w : w + 1, :]).astype(BF16)
        lhs_f[WIN * 64 :, :] = wgt[c]
        acc_f[...] += nt_dot(lhs_f[...], data[c])
        return carry

    lax.fori_loop(0, CHUNKS, late, 0)
    for w in range(WIN):
        w6 = i + w
        send_f[w6] = acc_f[w * 64 : w * 64 + 64, :].astype(BF16)
        send_p[w6] = acc_f[WIN * 64 + w : WIN * 64 + w + 1, :]
    f_cps = [
        remote(send_f.at[0:2], got_f.at[0], f_send.at[0], f_recv.at[0], lower),
        remote(send_f.at[4:6], got_f.at[1], f_send.at[1], f_recv.at[1], upper),
        remote(send_p.at[0:2], got_p.at[0], p_send.at[0], p_recv.at[0], lower),
        remote(send_p.at[4:6], got_p.at[1], p_send.at[1], p_recv.at[1], upper),
    ]
    for cp in f_cps:
        cp.start()
    for n in range(2):
        await_into(got_e.at[n], e_recv.at[n])
    for j in range(2):
        all_e[x, j] = (got_e[0, j].astype(F32) + got_e[1, j].astype(F32) + send_e[2 + j].astype(F32)).astype(BF16)
    eb_cps = [
        remote(all_e.at[x], all_e.at[x], eb_send.at[k - 1], eb_recv.at[k - 1], {"member": lax.rem(x + k, 4)})
        for k in (1, 3, 2)
    ]
    for cp in eb_cps:
        cp.start()

    for n in range(2):
        await_into(got_f.at[n], f_recv.at[n])
        await_into(got_p.at[n], p_recv.at[n])
    for j in range(2):
        all_f[x, j] = (got_f[0, j].astype(F32) + got_f[1, j].astype(F32) + send_f[2 + j].astype(F32)).astype(BF16)
        all_p[x, j] = got_p[0, j] + got_p[1, j] + send_p[2 + j]
    fb_cps = []
    for k in (1, 3, 2):
        fb_cps.append(
            remote(all_f.at[x], all_f.at[x], fb_send.at[k - 1], fb_recv.at[k - 1], {"member": lax.rem(x + k, 4)})
        )
        fb_cps.append(
            remote(all_p.at[x], all_p.at[x], pb_send.at[k - 1], pb_recv.at[k - 1], {"member": lax.rem(x + k, 4)})
        )
    for cp in fb_cps:
        cp.start()

    for cp in info_cps + [a2a(*args) for args in order] + e_cps + f_cps:
        cp.wait_send()

    def turn(value, xs):
        shift = (64 * (xs - 1)) % 256
        return pltpu.roll(value, shift, 1) if shift else value

    for k in (1, 3, 2):
        await_into(all_e.at[lax.rem(x + 4 - k, 4)], eb_recv.at[k - 1])
    side = jnp.zeros((64, 128), F32)
    for j in range(2):
        for r in range(4):
            a, b, c = (r + 1) % 4, r, (r + 3) % 4
            one = jnp.where(left, all_e[a, j, 0:64, :].astype(F32), 0.0)
            two = jnp.where(left, all_e[b, j, 64:128, :].astype(F32), all_e[b, j, 0:64, :].astype(F32))
            three = jnp.where(left, pltpu.roll(all_e[c, j, 64:128, :].astype(F32), 64, 1), 0.0)
            strip[j, 64 * r : 64 * r + 64, :] = (
                turn(jnp.concatenate([one, side], axis=1), a)
                + turn(jnp.concatenate([two, side], axis=1), b)
                + turn(jnp.concatenate([all_e[c, j, 128:192, :].astype(F32), three], axis=1), c)
            )
    off = lax.broadcasted_iota(jnp.int32, (256, 256), 0) // 64 != lax.broadcasted_iota(jnp.int32, (256, 256), 1) // 64
    for k in (1, 3, 2):
        src = lax.rem(x + 4 - k, 4)
        await_into(all_f.at[src], fb_recv.at[k - 1])
        await_into(all_p.at[src], pb_recv.at[k - 1])
    for j in range(2):
        proj = jnp.zeros((8, 256), F32)
        for r in range(4):
            far = (r + 2) % 4
            strip[j, 64 * r : 64 * r + 64, :] += turn(all_f[far, j].astype(F32), far)
            proj += turn(jnp.broadcast_to(all_p[r, j], (8, 256)), r)
        proj_out[j] = proj[0:1]
        whole = strip[j]
        gram_out[j] = whole + jnp.where(off, jnp.transpose(whole), 0.0)
    for cp in eb_cps + fb_cps:
        cp.wait_send()


def analysis_kernel(gram_ref, proj_ref, square_ref, root_ref, flat_ref, mean_ref, out_ref, tmp, done, out_sem):
    eye = (
        lax.broadcasted_iota(jnp.int32, (K, K), 0) == lax.broadcasted_iota(jnp.int32, (K, K), 1)
    ).astype(F32)
    grams = [split(gram_ref[t]) for t in range(2)]
    roots = [root_ref[0, t] for t in range(2)]
    for step in range(NEWTON):
        parts = [split(r) for r in roots]
        squares = [mm3(p, p) for p in parts] if step else [square_ref[t] for t in range(2)]
        sq_parts = [split(q) for q in squares]
        applied = [
            (K - 1.0) * squares[t] + mm3(grams[t], sq_parts[t]) for t in range(2)
        ]
        rest = [split(eye - a) for a in applied]
        roots = [roots[t] + 0.5 * mm3(parts[t], rest[t]) for t in range(2)]
    for t in range(2):
        root = roots[t]
        rh, rl = split(root)
        pr = jnp.broadcast_to(proj_ref[t], (8, K))
        ph, pl_ = split(pr)
        inner = (nt_dot(ph, rh) + (nt_dot(ph, rl) + nt_dot(pl_, rh)))[0:1]
        mean_weight = jnp.sum(root * inner, axis=1, keepdims=True)
        weights = (mean_weight + math.sqrt(K - 1) * root).astype(BF16)
        wt = jnp.transpose(weights)
        for two in range(4):
            res = mm(wt, flat_ref[t, :, two * 256 : (two + 1) * 256])
            for half in range(2):
                level = 2 * two + half
                tmp[t, pl.ds(level, K, stride=8), :] = (
                    res[:, half * 128 : (half + 1) * 128] + mean_ref[0, t, level : level + 1, :]
                )
        done[t] = tmp[t].reshape(K, 8, 128).astype(BF16)
        pltpu.make_async_copy(done.at[t], out_ref.at[0, t], out_sem.at[t]).start()
    for t in range(2):
        pltpu.make_async_copy(done.at[t], out_ref.at[0, t], out_sem.at[t]).wait()


def body(obs_anom, obs_prec, innov, obs_column, cutoff, inv_root, state_anom, state_mean):
    obs_anom, obs_prec, innov, obs_column, cutoff, state_anom, root_far = (
        pltpu.with_memory_space_constraint(a, pltpu.HBM)
        for a in (obs_anom, obs_prec, innov, obs_column, cutoff, state_anom, inv_root)
    )
    any_ = pl.BlockSpec(memory_space=pltpu.HBM)
    vm = pl.BlockSpec(memory_space=pltpu.VMEM)
    dma = pltpu.SemaphoreType.DMA
    gram, proj, flat, square = pl.pallas_call(
        gather_kernel,
        out_shape=(
            jax.ShapeDtypeStruct((2, K, K), F32),
            jax.ShapeDtypeStruct((2, 1, K), F32),
            jax.ShapeDtypeStruct((2, K, 1024), BF16),
            jax.ShapeDtypeStruct((2, K, K), F32),
        ),
        in_specs=[any_] * 7,
        out_specs=(vm,) * 4,
        scratch_shapes=[
            pltpu.VMEM((CHUNKS, K, WIDTH), BF16),
            pltpu.VMEM((2, 3, 2, 1024), BF16),
            pltpu.VMEM((2, 3, 2, 1024), BF16),
            pltpu.VMEM((2, 3, 2, 1024), jnp.int32),
            pltpu.SMEM((2, 128), jnp.int32),
            pltpu.VMEM((CHUNKS, 8, WIDTH), F32),
            pltpu.VMEM((CHUNKS, 16, WIDTH), BF16),
            pltpu.VMEM((WIN * NEAR, WIDTH), BF16),
            pltpu.VMEM((LATE, WIDTH), BF16),
            pltpu.VMEM((WIN * NEAR, 256), F32),
            pltpu.VMEM((LATE, K), F32),
            pltpu.VMEM((6, NEAR, 128), BF16),
            pltpu.VMEM((2, 2, NEAR, 128), BF16),
            pltpu.VMEM((6, 64, 256), BF16),
            pltpu.VMEM((2, 2, 64, 256), BF16),
            pltpu.VMEM((6, 1, 256), F32),
            pltpu.VMEM((2, 2, 1, 256), F32),
            pltpu.VMEM((4, 2, NEAR, 128), BF16),
            pltpu.VMEM((4, 2, 64, 256), BF16),
            pltpu.VMEM((4, 2, 1, 256), F32),
            pltpu.VMEM((2, K, K), F32),
            pltpu.VMEM((2, K, 8, 128), BF16),
            pltpu.VMEM((2, K, K), F32),
            pltpu.VMEM((128, 128), F32),
            dma((5,)),
            dma,
            dma((3,)),
            dma((3,)),
            dma((2, 4, 3)),
            dma((2, 4, 3)),
            *[dma((2,))] * 6,
            *[dma((3,))] * 6,
        ],
        compiler_params=pltpu.CompilerParams(
            collective_id=0, has_side_effects=True, vmem_limit_bytes=32 * 1024 * 1024
        ),
        name="gather",
    )(obs_anom, obs_prec, innov, obs_column, cutoff, state_anom, root_far)
    return pl.pallas_call(
        analysis_kernel,
        out_shape=jax.ShapeDtypeStruct(state_anom.shape, BF16),
        in_specs=[vm] * 6,
        out_specs=any_,
        scratch_shapes=[pltpu.VMEM((2, K * 8, 128), F32), pltpu.VMEM((2, K, 8, 128), BF16), dma((2,))],
        compiler_params=pltpu.CompilerParams(vmem_limit_bytes=32 * 1024 * 1024),
        name="analysis",
    )(gram, proj, square, inv_root, flat, state_mean)


def solution(mesh):
    in_specs = (
        P("tm", None, "space", "member", None),
        P("tm", None, "space", None),
        P("tm", None, "space", None),
        P("tm", None, "space", None),
        P(),
        P("tm", "space", None, None),
        P("tm", "space", None, "member", None),
        P("tm", "space", "member", None),
    )
    out_specs = P("tm", "space", None, "member", None)
    return jax.shard_map(body, mesh=mesh, in_specs=in_specs, out_specs=out_specs, check_vma=False)
```

time: 128 us -> 48.9 us (0.38)
  the two profiles are of different devices: /device:TPU:32 before, /device:TPU:8 now
where the time goes in v1:
time: 48.9 us; the launch traced here: 48.8 us
  Pallas kernels  48.8 us (100%)
    pallas_call x1, Pallas kernels, body(): pl.pallas_call(gather_kernel, out_shape=(jax.ShapeDtypeStruct((2, K, K),...  44.6 us
    pallas_call x1, Pallas kernels, body(): pl.pallas_call(analysis_kernel, out_shape=jax.ShapeDtypeStruct(state_anom...  4.14 us

profile of v1, /device:TPU:8, one launch (start us, length us, event | category | flops | bytes accessed | tf_op | source)
XLA Modules:
  0.0 48.8 jit_solution(17383654598102931588)
XLA Ops:
  0.0 0.0 copy-start
  0.0 0.0 copy-start.1
  0.0 44.6 %gather.1 = (f32[2,256,256]{2,1,0:T(8,128)S(1)}, f32[2,1,256]{2,1,0:T(1,128)S(1)}, bf16[2,256,1024]{2,1,0:T(8,128)(2,1)S(1)}, f32[2,256,256]{2,1,0:T(8,128)S(1)}) custom-call(bf16[3,2,2,64,1024]{4,3,2,1,0:T(8,128)(2,1)} %obs_ref.1, bf16[3,2,2,1024]{3,2,1,0:T(2,128)(2,1)} %prec_ref.1, bf16[3,2,2,1024]{3,2,1,0:T(2,128)(2,1)} %innov_ref.1, ...), custom_call_target="tpu_custom_call" | custom-call | tf_op jit(solution)/shard_map/gather/pallas_call | solution.py:347
  44.7 0.0 copy-done
  44.7 0.0 copy-done.1
  44.7 4.1 %analysis.1 = bf16[1,2,256,8,128]{4,3,2,1,0:T(8,128)(2,1)} custom-call(f32[2,256,256]{2,1,0:T(8,128)S(1)} %get-tuple-element.9.gram_ref, f32[2,1,256]{2,1,0:T(1,128)S(1)} %get-tuple-element.10.proj_ref, f32[2,256,256]{2,1,0:T(8,128)S(1)} %get-tuple-element.11.square_ref, f32[1,2,256,256]{3,2,1,0:T(8,128)S(1)} %copy-done, ...), custom_call_target="tpu_custom_call" | custom-call | tf_op jit(solution)/shard_map/analysis/pallas_call | solution.py:396
Async XLA Ops:
  0.0 44.7 %copy-start = (f32[1,2,256,256]{3,2,1,0:T(8,128)S(1)}, f32[1,2,256,256]{3,2,1,0:T(8,128)}, u32[]{:S(2)}) copy-start(f32[1,2,256,256]{3,2,1,0:T(8,128)} %root_ref.1) | copy-start | bytes 1572868
  0.0 44.7 %copy-start.1 = (f32[1,2,8,128]{3,2,1,0:T(8,128)S(1)}, f32[1,2,8,128]{3,2,1,0:T(8,128)}, u32[]{:S(2)}) copy-start(f32[1,2,8,128]{3,2,1,0:T(8,128)} %mean_ref.1) | copy-start | bytes 24580

commit v2 on v1

--- a/solution.py
+++ b/solution.py
@@ -15,6 +15,8 @@
 CHUNKS = 6
 WIDTH = 512
 WIN = 5
+TURN = 4
+RUN = 16
 NEAR = 192
 LATE = WIN * 64 + 16
 F32 = jnp.float32
@@ -42,7 +44,7 @@
 def gather_kernel(
     obs_ref, prec_ref, innov_ref, col_ref, cut_hbm, state_ref, root_hbm,
     gram_out, proj_out, flat_out, square_out,
-    data, prec_v, innov_v, col_v, cut_ref, coef, wgt, lhs_e, lhs_f, acc_e, acc_f,
+    turn_sem, data, prec_v, innov_v, col_v, cut_ref, coef, wgt, lhs_e, lhs_f, acc_e, acc_f,
     send_e, got_e, send_f, got_f, send_p, got_p, all_e, all_f, all_p, strip, state_v, root_v, tmp,
     info_sem, state_sem, info_send, info_recv, a2a_send, a2a_recv,
     e_send, e_recv, f_send, f_recv, p_send, p_recv, eb_send, eb_recv, fb_send, fb_recv, pb_send, pb_recv,
@@ -126,8 +128,14 @@
 
     order = [(h, k, c) for c in range(3) for h, k in ((0, 1), (0, 3), (1, 0), (1, 1), (1, 3))]
     order += [(h, 2, c) for c in range(3) for h in range(2)]
-    for args in order:
-        a2a(*args).start()
+
+    def send_all():
+        for args in order:
+            a2a(*args).start()
+
+    hurried = lax.rem(s, RUN) == RUN - 1
+    held = lax.rem(s, RUN) == RUN - 2
+    pl.when(jnp.logical_not(held))(send_all)
 
     z6 = jnp.where(i == 0, 5, 0)
     send_e[z6] = jnp.zeros((NEAR, 128), BF16)
@@ -178,6 +186,11 @@
         part = split(root_v[t])
         square_out[t] = mm3(part, part)
 
+    @pl.when(held)
+    def _():
+        pl.semaphore_wait(turn_sem, 1)
+        send_all()
+
     acc_e[...] = jnp.zeros_like(acc_e)
     acc_f[...] = jnp.zeros_like(acc_f)
 
@@ -190,6 +203,11 @@
             for w in range(WIN):
                 lhs_e[w * NEAR + rb * 32 : w * NEAR + (rb + 1) * 32, :] = (rows * coef[c, w : w + 1, :]).astype(BF16)
         acc_e[:, 0:NEAR] += nt_dot(lhs_e[...], data[c, 0:NEAR, :])
+
+        @pl.when(hurried & (c == TURN))
+        def _():
+            pl.semaphore_signal(turn_sem, inc=1, device_id={"space": s - 1}, device_id_type=MESH)
+
         return carry
 
     lax.fori_loop(0, CHUNKS, near, 0)
@@ -312,8 +330,8 @@
         applied = [
             (K - 1.0) * squares[t] + mm3(grams[t], sq_parts[t]) for t in range(2)
         ]
-        rest = [split(eye - a) for a in applied]
-        roots = [roots[t] + 0.5 * mm3(parts[t], rest[t]) for t in range(2)]
+        rest = [(0.5 * (eye - a)).astype(BF16) for a in applied]
+        roots = [roots[t] + mm(parts[t][0], rest[t]) for t in range(2)]
     for t in range(2):
         root = roots[t]
         rh, rl = split(root)
@@ -355,6 +373,7 @@
         in_specs=[any_] * 7,
         out_specs=(vm,) * 4,
         scratch_shapes=[
+            pltpu.SemaphoreType.REGULAR,
             pltpu.VMEM((CHUNKS, K, WIDTH), BF16),
             pltpu.VMEM((2, 3, 2, 1024), BF16),
             pltpu.VMEM((2, 3, 2, 1024), BF16),

time: 48.9 us -> 43.3 us (0.89)
  Pallas kernels: 48.8 us -> 43.1 us
    pallas_call x1, Pallas kernels: 44.6 us -> 39.3 us  [body(): pl.pallas_call(gather_kernel, out_shape=(jax.ShapeDtypeStruct((2, K, K),...]
where the time goes in v2:
time: 43.3 us; the launch traced here: 43.2 us
  Pallas kernels  43.1 us (100%)
    pallas_call x1, Pallas kernels, body(): pl.pallas_call(gather_kernel, out_shape=(jax.ShapeDtypeStruct((2, K, K),...  39.3 us
    pallas_call x1, Pallas kernels, body(): pl.pallas_call(analysis_kernel, out_shape=jax.ShapeDtypeStruct(state_anom...  3.8 us

profile of v2, /device:TPU:8, one launch (start us, length us, event | category | flops | bytes accessed | tf_op | source)
XLA Modules:
  0.0 43.2 jit_solution(930351256784047292)
XLA Ops:
  0.0 0.0 copy-start
  0.0 0.0 copy-start.1
  0.0 39.3 %gather.1 = (f32[2,256,256]{2,1,0:T(8,128)S(1)}, f32[2,1,256]{2,1,0:T(1,128)S(1)}, bf16[2,256,1024]{2,1,0:T(8,128)(2,1)S(1)}, f32[2,256,256]{2,1,0:T(8,128)S(1)}) custom-call(bf16[3,2,2,64,1024]{4,3,2,1,0:T(8,128)(2,1)} %obs_ref.1, bf16[3,2,2,1024]{3,2,1,0:T(2,128)(2,1)} %prec_ref.1, bf16[3,2,2,1024]{3,2,1,0:T(2,128)(2,1)} %innov_ref.1, ...), custom_call_target="tpu_custom_call" | custom-call | tf_op jit(solution)/shard_map/gather/pallas_call | solution.py:365
  39.4 0.0 copy-done
  39.4 0.0 copy-done.1
  39.4 3.8 %analysis.1 = bf16[1,2,256,8,128]{4,3,2,1,0:T(8,128)(2,1)} custom-call(f32[2,256,256]{2,1,0:T(8,128)S(1)} %get-tuple-element.9.gram_ref, f32[2,1,256]{2,1,0:T(1,128)S(1)} %get-tuple-element.10.proj_ref, f32[2,256,256]{2,1,0:T(8,128)S(1)} %get-tuple-element.11.square_ref, f32[1,2,256,256]{3,2,1,0:T(8,128)S(1)} %copy-done, ...), custom_call_target="tpu_custom_call" | custom-call | tf_op jit(solution)/shard_map/analysis/pallas_call | solution.py:415
Async XLA Ops:
  0.0 39.4 %copy-start = (f32[1,2,256,256]{3,2,1,0:T(8,128)S(1)}, f32[1,2,256,256]{3,2,1,0:T(8,128)}, u32[]{:S(2)}) copy-start(f32[1,2,256,256]{3,2,1,0:T(8,128)} %root_ref.1) | copy-start | bytes 1572868
  0.0 39.4 %copy-start.1 = (f32[1,2,8,128]{3,2,1,0:T(8,128)S(1)}, f32[1,2,8,128]{3,2,1,0:T(8,128)}, u32[]{:S(2)}) copy-start(f32[1,2,8,128]{3,2,1,0:T(8,128)} %mean_ref.1) | copy-start | bytes 24580
